TPU v7x, 32 devices: a whole 2x2x4 slice. The times are simulated.
32 devices in a mesh: seq: 8 (over y, x, core), heads: 4 (over z).
Axes of the slice: x: 2, y: 2, z: 4, core: 2. Of those that a mesh axis runs over, the one named last changes fastest.
Arguments:
- queries: bfloat16 [2048, 16, 128], P('seq', 'heads'), may hold values from -6 to 6
- key_vecs: bfloat16 [2048, 16, 128], P('seq', 'heads'), may hold values from -12 to 12
- values: bfloat16 [2048, 32, 128], P('seq', 'heads'), may hold values from -6 to 6
- strength: float32 [2048, 32], P('seq', 'heads'), may hold values from 0 to 1, as said below
- decay_rate: float32 [2048, 32], P('seq', 'heads'), may hold values from 0 to 0.15, as said below
- norm_gain: float32 [128], replicated, may hold values from 0.5 to 1.5
- w_out: bfloat16 [4096, 2048], P('heads'), may hold values from -0.09375 to 0.09375
Outputs:
- mixed: bfloat16 [2048, 2048], P(('seq', 'heads'))
Inputs may be any that keep to these rules, and one draw needn't show every extreme that they name: Every write strength lies strictly between 0 and 1. `decay_rate`: every decay rate is positive.
All inputs are finite; a program needn't handle non-finite values.
Results may differ from a plain program's by a relative error of at most 0.0049.
Values sent between devices are 32-bit elements; how exact they have to be, the bound alone decides.
A program may use at most 192 MiB of HBM per device.

v0:
```python
import jax
import jax.numpy as jnp
from jax import lax
from jax.sharding import PartitionSpec as P

BLOCK_TOKENS = 64


strict_precision = lax.Precision.HIGHEST
norm_eps = 1e-12
unit_eps = 1e-06


def entering(value, axis, join, neutral):
    count, mine = (lax.axis_size(axis), lax.axis_index(axis))
    pieces = jax.tree.map(lambda part: lax.all_gather(part, axis), value)
    running = jax.tree.map(
        lambda part, zero: jnp.full_like(part, 0) + jnp.asarray(zero, part.dtype), value, neutral
    )

    def lap(position, running):
        longer = join(running, jax.tree.map(lambda part: part[position], pieces))
        return jax.tree.map(lambda new, old: jnp.where(position < mine, new, old), longer, running)

    return lax.fori_loop(0, count - 1, lap, running)


def unit_rows(matrix):
    matrix = matrix.astype(jnp.float32)
    return matrix / jnp.sqrt(jnp.sum(matrix * matrix, axis=-1, keepdims=True) + unit_eps)


def prepare(query_blk, key_blk, value_blk, strength_blk, decay_blk):
    group_size = value_blk.shape[1] // query_blk.shape[1]
    normalized_queries = jnp.repeat(
        jnp.transpose(unit_rows(query_blk), (1, 0, 2)), group_size, axis=0
    )
    keys_n = jnp.repeat(jnp.transpose(unit_rows(key_blk), (1, 0, 2)), group_size, axis=0)
    values_f = jnp.transpose(value_blk.astype(jnp.float32), (1, 0, 2))
    writes = jnp.transpose(strength_blk)
    decay_logarithm = -jnp.cumsum(jnp.transpose(decay_blk), axis=1)
    return (normalized_queries, keys_n, values_f, writes, decay_logarithm)


def block_parts(normalized_queries, keys_n, values_f, writes, decay_logarithm):
    key_width = keys_n.shape[2]
    length = keys_n.shape[1]
    row_ids = lax.broadcasted_iota(jnp.int32, (length, length), 0)
    col_ids = lax.broadcasted_iota(jnp.int32, (length, length), 1)
    ratios = jnp.exp(jnp.minimum(decay_logarithm[:, :, None] - decay_logarithm[:, None, :], 0.0))
    key_dots = jnp.einsum("hik,hjk->hij", keys_n, keys_n, precision=strict_precision)
    query_dots = jnp.einsum("hik,hjk->hij", normalized_queries, keys_n, precision=strict_precision)
    system = jnp.where(row_ids > col_ids, writes[:, :, None] * ratios * key_dots, 0.0)
    system = system + jnp.eye(length, dtype=jnp.float32)
    scaled = writes * jnp.exp(decay_logarithm)
    right_side = jnp.concatenate(
        [scaled[:, :, None] * keys_n, writes[:, :, None] * values_f], axis=2
    )
    solved = jax.scipy.linalg.solve_triangular(system, right_side, lower=True, unit_diagonal=True)
    weighted_key_rows = solved[:, :, :key_width]
    corrected_values = solved[:, :, key_width:]
    mixing = jnp.where(row_ids >= col_ids, ratios * query_dots, 0.0)
    trailing_keys = jnp.exp(decay_logarithm[:, -1:] - decay_logarithm)[:, :, None] * keys_n
    return (weighted_key_rows, corrected_values, mixing, trailing_keys)


def block_apply(
    memory_state,
    normalized_queries,
    decay_logarithm,
    weighted_key_rows,
    corrected_values,
    mixing,
    trailing_keys,
):
    state_increment = corrected_values - jnp.einsum(
        "qjl,qlo->qjo", weighted_key_rows, memory_state, precision=strict_precision
    )
    output_rows = jnp.exp(decay_logarithm)[:, :, None] * jnp.einsum(
        "qjl,qlo->qjo", normalized_queries, memory_state, precision=strict_precision
    )
    output_rows = output_rows + jnp.einsum(
        "hij,hjv->hiv", mixing, state_increment, precision=strict_precision
    )
    updated_state = jnp.exp(decay_logarithm[:, -1])[:, None, None] * memory_state
    updated_state = updated_state + jnp.einsum(
        "oqm,oqy->omy", trailing_keys, state_increment, precision=strict_precision
    )
    return (updated_state, output_rows)


def normalize(output_rows, norm_gain):
    mean_sq = jnp.mean(output_rows * output_rows, axis=-1, keepdims=True)
    return (output_rows / jnp.sqrt(mean_sq + norm_eps) * norm_gain).astype(jnp.bfloat16)


def compose_maps(transit_all, offset_all):

    def fold_maps(carried, map_pair):
        transit, block_displacement = map_pair
        matrix = jnp.einsum("hij,hjk->hik", transit, carried[0], precision=strict_precision)
        shifted = (
            jnp.einsum("hij,hjv->hiv", transit, carried[1], precision=strict_precision)
            + block_displacement
        )
        return ((matrix, shifted), None)

    first_shape = transit_all.shape[1:]
    initial = (
        jnp.broadcast_to(jnp.eye(first_shape[1], dtype=jnp.float32), first_shape),
        jnp.zeros(offset_all.shape[1:], jnp.float32),
    )
    result, _ = lax.scan(fold_maps, initial, (transit_all, offset_all))
    return result


def chain_maps(earlier_map, later_map):
    matrix = jnp.einsum("hij,hjk->hik", later_map[0], earlier_map[0], precision=strict_precision)
    shifted = (
        jnp.einsum("hij,hjv->hiv", later_map[0], earlier_map[1], precision=strict_precision)
        + later_map[1]
    )
    return (matrix, shifted)


def identity_of(composed):
    return (
        jnp.broadcast_to(jnp.eye(composed[0].shape[1], dtype=jnp.float32), composed[0].shape),
        jnp.zeros_like(composed[1]),
    )


def body(queries, key_vecs, values, strength, decay_rate, norm_gain, w_out):
    local_len = queries.shape[0]
    block_count = local_len // BLOCK_TOKENS
    heads_v = values.shape[1]
    key_width = key_vecs.shape[2]
    value_width = values.shape[2]
    blocks = (
        queries.reshape(block_count, BLOCK_TOKENS, queries.shape[1], key_width),
        key_vecs.reshape(block_count, BLOCK_TOKENS, key_vecs.shape[1], key_width),
        values.reshape(block_count, BLOCK_TOKENS, heads_v, value_width),
        strength.reshape(block_count, BLOCK_TOKENS, heads_v),
        decay_rate.reshape(block_count, BLOCK_TOKENS, heads_v),
    )

    def analyse(carried, pieces):
        prepared = prepare(pieces[0], pieces[1], pieces[2], pieces[3], pieces[4])
        weighted_key_rows, corrected_values, mixing, trailing_keys = block_parts(*prepared)
        block_decay = jnp.exp(prepared[4][:, -1])
        transit = block_decay[:, None, None] * jnp.eye(key_width, dtype=jnp.float32)
        transit = transit - jnp.einsum(
            "hck,hcj->hkj", trailing_keys, weighted_key_rows, precision=strict_precision
        )
        block_displacement = jnp.einsum(
            "oqm,oqy->omy", trailing_keys, corrected_values, precision=strict_precision
        )
        stored = (
            prepared[0],
            prepared[4],
            weighted_key_rows,
            corrected_values,
            mixing,
            trailing_keys,
        )
        return (carried, (stored, (transit, block_displacement)))

    _, (stored_all, map_pairs) = lax.scan(analyse, jnp.zeros((), jnp.float32), blocks)
    transit_all, offset_all = map_pairs
    composed = compose_maps(transit_all, offset_all)
    earlier = entering(composed, "seq", chain_maps, identity_of(composed))
    incoming = earlier[1]

    def emit(memory_state, stored):
        updated_state, output_rows = block_apply(
            memory_state, stored[0], stored[1], stored[2], stored[3], stored[4], stored[5]
        )
        return (updated_state, normalize(jnp.transpose(output_rows, (1, 0, 2)), norm_gain))

    _, normed = lax.scan(emit, incoming, stored_all)
    flat = normed.reshape(local_len, heads_v * value_width)
    mixed = lax.psum_scatter(
        jnp.dot(flat, w_out, preferred_element_type=jnp.float32),
        "heads",
        scatter_dimension=0,
        tiled=True,
    )
    return mixed.astype(jnp.bfloat16)


def solution(mesh):
    return jax.shard_map(
        body,
        mesh=mesh,
        in_specs=(
            P("seq", "heads", None),
            P("seq", "heads", None),
            P("seq", "heads", None),
            P("seq", "heads"),
            P("seq", "heads"),
            P(),
            P("heads", None),
        ),
        out_specs=P(("seq", "heads"), None),
        check_vma=False,
    )
```

profile of v0, /device:TPU:22, one launch (start us, length us, event | category | flops | bytes accessed | tf_op | source)
XLA Modules:
  0.0 408.1 jit_solution(16902464041056474408)
XLA Ops:
  8.1 214.5 %while.63 = (s32[]{:T(128)}, f32[4,8,64,128]{3,2,1,0:T(8,128)}, f32[4,8,64]{2,1,0:T(8,128)S(1)}, f32[4,8,64,128]{3,2,1,0:T(8,128)}, f32[4,8,64,128]{3,2,1,0:T(8,...) while((s32[]{:T(128)}, f32[4,8,64,128]{3,2,1,0:T(8,128)}, ...), condition=%wide.region_4.5_spmd, body=%wide.region_0.4_spmd.sunk | while | flops 404191296 | bytes 9727317 | solution.py:168
  11.4 40.7 %custom-call.16 = f32[8,1,64,64]{2,3,1,0:T(8,128)} custom-call(f32[8,1,64,64]{3,2,1,0:T(8,128)} %fusion.137), custom_call_target="InvertDiagBlocksLowerTriangular" | custom-call | tf_op jit(solution)/shard_map/while/body/eval_jaxpr/jit(_solve_triangular)/vmap()/triangular_solve | solution.py:59
  53.1 1.6 fusion.138
  56.8 1.8 fusion.142
  65.0 40.7 %custom-call.16 = f32[8,1,64,64]{2,3,1,0:T(8,128)} custom-call(f32[8,1,64,64]{3,2,1,0:T(8,128)} %fusion.137), custom_call_target="InvertDiagBlocksLowerTriangular" | custom-call | tf_op jit(solution)/shard_map/while/body/eval_jaxpr/jit(_solve_triangular)/vmap()/triangular_solve | solution.py:59
  106.8 1.6 fusion.138
  110.4 1.8 fusion.142
  118.7 40.7 %custom-call.16 = f32[8,1,64,64]{2,3,1,0:T(8,128)} custom-call(f32[8,1,64,64]{3,2,1,0:T(8,128)} %fusion.137), custom_call_target="InvertDiagBlocksLowerTriangular" | custom-call | tf_op jit(solution)/shard_map/while/body/eval_jaxpr/jit(_solve_triangular)/vmap()/triangular_solve | solution.py:59
  160.4 1.6 fusion.138
  164.0 1.8 fusion.142
  172.3 40.7 %custom-call.16 = f32[8,1,64,64]{2,3,1,0:T(8,128)} custom-call(f32[8,1,64,64]{3,2,1,0:T(8,128)} %fusion.137), custom_call_target="InvertDiagBlocksLowerTriangular" | custom-call | tf_op jit(solution)/shard_map/while/body/eval_jaxpr/jit(_solve_triangular)/vmap()/triangular_solve | solution.py:59
  214.0 1.6 fusion.138
  217.7 1.8 fusion.142
  222.7 9.9 %while.65 = (s32[]{:T(128)}, f32[8,128,128]{2,1,0:T(8,128)S(1)}, f32[8,128,128]{2,1,0:T(8,128)S(1)}, f32[4,8,128,128]{3,2,1,0:T(8,128)S(1)}, f32[4,8,128,128]{3,2,1,0:T(8,128)}, /*index=5*/s32[]{:T(128)}, s32[]{:T(128)}) while((s32[]{:T(128)}, f32[8,128,128]{2,1,0:T(8,128)S(1)}, f32[8,128,128]{2,1,0:T(8,128)S(1)}, ...), condition=%wide.region_6.7_spmd.clone, body=%wide.region_5.6_spmd.clone.sunk | while | flops 402915328 | bytes 5768283 | solution.py:113
  222.7 1.7 convolution_add_fusion.6
  225.2 1.7 convolution_add_fusion.6
  227.7 1.7 convolution_add_fusion.6
  230.1 1.7 convolution_add_fusion.6
  234.2 36.0 %all-gather.5.cloned.1.call-done = f32[64,128,128]{2,1,0:T(8,128)} async-done(((f32[8,128,128]{2,1,0:T(8,128)}), f32[64,128,128]{2,1,0:T(8,128)}) %all-gather.5.cloned.1.call-update) | async-done | bytes 4194320 | tf_op jit(solution)/shard_map/all_gather | solution.py:16
  270.2 38.5 %all-gather.7.cloned.1.call-done = f32[64,128,128]{2,1,0:T(8,128)} async-done(((f32[8,128,128]{2,1,0:T(8,128)}), f32[64,128,128]{2,1,0:T(8,128)}) %all-gather.7.cloned.1.call-update) | async-done | bytes 4194320 | tf_op jit(solution)/shard_map/all_gather | solution.py:16
  308.7 13.6 %while.66 = (s32[]{:T(128)}, f32[8,128,128]{2,1,0:T(8,128)S(1)}, s32[]{:T(128)}, f32[8,8,128,128]{3,2,1,0:T(8,128)}, f32[8,8,128,128]{3,2,1,0:T(8,128)}, /*index=5*/s32[]{:T(128)}, s32[]{:T(128)}) while((s32[]{:T(128)}, f32[8,128,128]{2,1,0:T(8,128)S(1)}, s32[]{:T(128)}, f32[8,8,128,128]{3,2,1,0:T(8,128)}, ...), condition=%wide.region_8.9_spmd.clone, body=%wide.region_7.8_spmd.clone.sunk | while | flops 201850880 | bytes 3672671 | solution.py:25
  308.7 1.9 fusion.160
  310.7 1.9 fusion.160
  312.6 1.9 fusion.160
  314.6 1.9 fusion.160
  316.5 1.9 fusion.160
  318.5 1.9 fusion.160
  320.4 1.9 fusion.160
  322.3 28.8 %while.64 = (s32[]{:T(128)}, f32[8,128,128]{2,1,0:T(8,128)S(1)}, bf16[4,64,8,128]{3,2,1,0:T(8,128)(2,1)S(1)}, f32[4,8,64]{2,1,0:T(8,128)S(1)}, f32[4,8,64,128]{3...) while((s32[]{:T(128)}, f32[8,128,128]{2,1,0:T(8,128)S(1)}, ...), condition=%wide.region_11.12_spmd, body=%wide.region_9.11_spmd.sunk | while | flops 353108480 | bytes 5666005 | solution.py:180
  322.5 1.6 fusion.151
  324.0 1.6 convolution_subtract_fusion.3
  325.7 1.5 multiply_reduce_fusion.2
  327.4 2.1 convolution_add_fusion.5
  329.7 1.6 fusion.151
  331.2 1.6 convolution_subtract_fusion.3
  332.9 1.5 multiply_reduce_fusion.2
  334.6 2.1 convolution_add_fusion.5
  336.9 1.6 fusion.151
  338.4 1.6 convolution_subtract_fusion.3
  340.1 1.5 multiply_reduce_fusion.2
  341.8 2.1 convolution_add_fusion.5
  344.1 1.6 fusion.151
  345.6 1.6 convolution_subtract_fusion.3
  347.3 1.5 multiply_reduce_fusion.2
  349.0 2.1 convolution_add_fusion.5
  351.1 4.8 %fusion.63 = f32[256,2048]{1,0:T(8,128)} fusion(bf16[1024,2048]{1,0:T(8,128)(2,1)} %param.21, bf16[32,8,8,128]{3,2,1,0:T(8,128)(2,1)S(1)} %bitcast.252), kind=kOutput, calls=%fused_computation.113 | convolution fusion | flops 1073741824 | bytes 6815744 | tf_op jit(solution)/shard_map/dot_general | solution.py:183
  355.9 43.9 %reduce-scatter.2.cloned.1.call-done = f32[64,2048]{1,0:T(8,128)} async-done(((f32[256,2048]{1,0:T(8,128)}), f32[64,2048]{1,0:T(8,128)}) %reduce-scatter.2.cloned.1.call-update) | async-done | bytes 524304 | tf_op jit(solution)/shard_map/reduce_scatter | solution.py:182
  399.8 1.8 convert_element_type.40
  (210 shorter events, 45.6 us)
Async XLA Ops:
  6.5 263.6 %all-gather.5.cloned.1.call-start = ((), (), s32[]{:S(2)}) async-start(), calls=%async_computation.2 | async-start | bytes 4718592 | tf_op jit(solution)/shard_map/all_gather | solution.py:16
  232.6 0.8 copy-start
  232.6 1.0 copy-start.1
  233.4 75.3 %all-gather.7.cloned.1.call-start = ((), (), s32[]{:S(2)}) async-start(), calls=%async_computation.3 | async-start | bytes 4718592 | tf_op jit(solution)/shard_map/all_gather | solution.py:16
  234.1 165.7 %reduce-scatter.2.cloned.1.call-start = ((), (), s32[]{:S(2)}) async-start(), calls=%async_computation.1 | async-start | bytes 2621440 | tf_op jit(solution)/shard_map/reduce_scatter | solution.py:182
  308.7 13.6 %copy-start.2 = (f32[128]{0:T(128)S(1)}, f32[128]{0:T(128)}, u32[]{:S(2)}) copy-start(f32[128]{0:T(128)} %param.20) | copy-start | bytes 1540
Sparse Core Ops, SparseCore 0:
  233.5 36.6 all-gather.4
  272.1 36.5 all-gather.6
  356.0 43.7 reduce-scatter.1
where the time goes:
time: 413 us; the launch traced here: 408 us
  other arithmetic  174 us (42%)
  waiting for transfers between devices  119 us (29%)
  matrix products  81.9 us (20%)
  local copies, waits for them, and re-layouts  18.6 us (5%)
  between operations  13.2 us (3%)
    another operation x16, other arithmetic, block_parts(): jax.scipy.linalg.solve_triangular(system, right_side, lower=True, unit_di...  163 us
    all_gather x2, waiting for transfers between devices, entering(): pieces = jax.tree.map(lambda part: lax.all_gather(part, axis), value)  74.5 us
    reduce_scatter x1, waiting for transfers between devices, body(): lax.psum_scatter(jnp.dot(flat, w_out, preferred_element_type=jnp.float32)...  43.9 us
    dot_general x7, matrix products, chain_maps(): jnp.einsum('hij,hjv->hiv', later_map[0], earlier_map[1], precision=strict...  13.1 us
    dynamic_slice x20, local copies, waits for them, and re-layouts, body(): lax.scan(analyse, jnp.zeros((), jnp.float32), blocks)  10.7 us
  transfers between devices with their start and end apart: 3, of which 3 were waited for; matrix products, arithmetic and copies ran while one was open for 0% of the time, Pallas kernels for 0%

commit v1 on v0

v1 whole, which is shorter than its diff:
```python
import functools

import jax
import jax.numpy as jnp
from jax import lax
from jax.experimental import pallas as pl
from jax.experimental.pallas import tpu as pltpu
from jax.sharding import PartitionSpec as P

norm_eps = 1e-12
unit_eps = 1e-06
BASE = 16
HALF = 128
f32, bf16 = jnp.float32, jnp.bfloat16

NN = (((1,), (0,)), ((), ()))
NT = (((1,), (1,)), ((), ()))
TN = (((0,), (0,)), ((), ()))


def mm(a, b, dims=NN):
    return lax.dot_general(a, b, dims, preferred_element_type=f32)


def split(x):
    high = x.astype(bf16)
    return high, (x - high.astype(f32)).astype(bf16)


def split3(x):
    high = x.astype(bf16)
    rest = x - high.astype(f32)
    mid = rest.astype(bf16)
    return high, mid, (rest - mid.astype(f32)).astype(bf16)


def mm3(a, b, dims=NN):
    return mm(a[0], b[0], dims) + (mm(a[0], b[1], dims) + mm(a[1], b[0], dims))


def iota(shape, dim):
    return lax.broadcasted_iota(jnp.int32, shape, dim)


def diagonal_inverses(systems, length):
    count = length // BASE
    lane = iota((BASE, length), 1)
    packed = []
    for low in systems:
        rows = jnp.zeros((BASE, length), f32)
        for b in range(count):
            rows = rows + jnp.where(lane // BASE == b, low[b * BASE : (b + 1) * BASE], 0.0)
        packed.append(rows)
    packed = jnp.concatenate(packed, axis=0)
    total = packed.shape[0]
    parts = []
    for start in range(0, length, 128):
        chunk = packed[:, start : start + 128]
        group = iota((total, 128), 1) // BASE * BASE
        local = iota((total, 128), 1) % BASE
        parts.append((chunk, group))
    outs = []
    for chunk, group in parts:
        solved = [
            jnp.where(iota((BASE, 128), 0) == iota((BASE, 128), 1) % BASE, 1.0, 0.0).astype(f32)
            for _ in systems
        ]
        for j in range(BASE - 1):
            column = jnp.take_along_axis(chunk, group + j, axis=1)
            solved = [
                x - column[n * BASE : (n + 1) * BASE] * x[j : j + 1] for n, x in enumerate(solved)
            ]
        outs.append(solved)
    return [[outs[c][n] for c in range(len(outs))] for n in range(len(systems))]


def spread(block):
    lane = iota((BASE, HALF), 1)
    return jnp.concatenate(
        [jnp.where(lane // BASE == b, block, 0.0) for b in range(HALF // BASE)], axis=0
    )


def local_kernel(
    group_size, q_ref, k_ref, v_ref, strength_ref, decay_ref, transit_ref, offset_ref, reach_ref, near_ref
):
    step = pl.program_id(0)
    length = q_ref.shape[0]
    heads = decay_ref.shape[1]
    width = k_ref.shape[1]
    query, key = q_ref[...], k_ref[...]
    query_f, key_f = query.astype(f32), key.astype(f32)
    query_scale = lax.rsqrt(jnp.sum(query_f * query_f, axis=1, keepdims=True) + unit_eps)
    key_sq = key_f * key_f
    key_scale = lax.rsqrt(jnp.sum(key_sq, axis=1, keepdims=True) + unit_eps)
    ones = jnp.ones((8, width), bf16)
    sq_high, sq_low = split(key_sq)
    key_scale_row = lax.rsqrt(mm(ones, sq_high, NT)[:1] + mm(ones, sq_low, NT)[:1] + unit_eps)

    row, col = iota((length, length), 0), iota((length, length), 1)
    lower = jnp.where(row >= col, 1.0, 0.0).astype(bf16)
    upper = jnp.where(row <= col, 1.0, 0.0).astype(bf16)
    pieces = split3(-decay_ref[...])
    logs = mm(lower, pieces[0]) + (mm(lower, pieces[1]) + mm(lower, pieces[2]))
    logs_row = mm(pieces[0], upper, TN) + (mm(pieces[1], upper, TN) + mm(pieces[2], upper, TN))

    key_dots = mm(key, key, NT) * key_scale * key_scale_row
    query_dots = mm(query, key, NT) * query_scale * key_scale_row

    half = [slice(s, s + HALF) for s in range(0, length, HALF)]
    systems, mixings, log_cols, writes = [], [], [], []
    for n in range(group_size):
        head = step * group_size + n
        lane = iota((length, heads), 1)
        log_col = jnp.sum(jnp.where(lane == head, logs, 0.0), axis=1, keepdims=True)
        write = jnp.sum(jnp.where(lane == head, strength_ref[...], 0.0), axis=1, keepdims=True)
        log_row = jnp.sum(
            jnp.where(iota((heads, length), 0) == head, logs_row, 0.0), axis=0, keepdims=True
        )
        ratio = jnp.exp(jnp.minimum(log_col - log_row, 0.0))
        systems.append(jnp.where(row > col, write * ratio * key_dots, 0.0))
        mixings.append(jnp.where(row >= col, ratio * query_dots, 0.0))
        log_cols.append(log_col)
        writes.append(write)

    base = diagonal_inverses(systems, length)
    r, c = iota((HALF, HALF), 0), iota((HALF, HALF), 1)
    units = [(n, s) for n in range(group_size) for s in range(len(half))]
    inverse = {u: spread(base[u[0]][u[1]]) for u in units}
    size = BASE
    while size < HALF:
        joint = (r // (2 * size) == c // (2 * size)) & (r // size > c // size)
        halves = {u: split(inverse[u]) for u in units}
        between = {
            u: mm3(split(jnp.where(joint, systems[u[0]][half[u[1]], half[u[1]]], 0.0)), halves[u])
            for u in units
        }
        inverse = {u: inverse[u] - mm3(halves[u], split(between[u])) for u in units}
        size *= 2
    inverse = {u: split(inverse[u]) for u in units}

    solved = [[] for _ in range(group_size)]
    for s in range(len(half)):
        for n in range(group_size):
            write = writes[n][half[s]]
            key_part = (write * jnp.exp(log_cols[n][half[s]]) * key_scale[half[s]]) * key_f[half[s]]
            value_part = write * v_ref[half[s], n * width : (n + 1) * width].astype(f32)
            right = jnp.concatenate([key_part, value_part], axis=1)
            if s:
                done = split(jnp.concatenate(solved[n], axis=0))
                right = right - mm3(split(systems[n][half[s], : s * HALF]), done)
            solved[n].append(mm3(inverse[n, s], split(right)))

    eye = jnp.where(r == c, 1.0, 0.0)
    for n in range(group_size):
        full = split(jnp.concatenate(solved[n], axis=0))
        log_col = log_cols[n]
        mixed = mm3(split(mixings[n]), full)
        reach = (jnp.exp(log_col) * query_scale) * query_f - mixed[:, :width]
        reach_ref[n] = reach
        near_ref[n] = mixed[:, width:]
        last = log_col[length - 1 :]
        trailing = split((jnp.exp(last - log_col) * key_scale) * key_f)
        maps = mm3(trailing, full, TN)
        transit_ref[n] = jnp.exp(last) * eye - maps[:, :width]
        offset_ref[n] = maps[:, width:]


def local_phase(queries, key_vecs, values, strength, decay_rate, interpret=False):
    length, heads_k, width = queries.shape
    heads_v = values.shape[1]
    group_size = heads_v // heads_k
    per_head = lambda rows: pl.BlockSpec((group_size, rows, width), lambda i: (i, 0, 0))
    lanes = lambda n: pl.BlockSpec((length, n * width), lambda i: (0, i))
    whole = pl.BlockSpec((length, heads_v), lambda i: (0, 0))
    return pl.pallas_call(
        functools.partial(local_kernel, group_size),
        grid=(heads_k,),
        in_specs=[lanes(1), lanes(1), lanes(group_size), whole, whole],
        out_specs=[per_head(width), per_head(width), per_head(length), per_head(length)],
        out_shape=[
            jax.ShapeDtypeStruct((heads_v, width, width), f32),
            jax.ShapeDtypeStruct((heads_v, width, width), f32),
            jax.ShapeDtypeStruct((heads_v, length, width), f32),
            jax.ShapeDtypeStruct((heads_v, length, width), f32),
        ],
        interpret=interpret,
        name="local_phase",
    )(
        queries.reshape(length, heads_k * width),
        key_vecs.reshape(length, heads_k * width),
        values.reshape(length, heads_v * width),
        strength,
        decay_rate,
    )


def batched3(a, b):
    one = lambda x, y: jnp.einsum("hik,hkj->hij", x, y, preferred_element_type=f32)
    a, b = split(a), split(b)
    return one(a[0], b[0]) + (one(a[0], b[1]) + one(a[1], b[0]))


def body(queries, key_vecs, values, strength, decay_rate, norm_gain, w_out):
    length = queries.shape[0]
    transit, offset, reach, near = local_phase(queries, key_vecs, values, strength, decay_rate)
    count, mine = lax.axis_size("seq"), lax.axis_index("seq")
    maps = lax.all_gather(jnp.concatenate([transit, offset], axis=2), "seq")
    width = transit.shape[1]

    def lap(position, state):
        pair = maps[position]
        longer = batched3(pair[:, :, :width], state) + pair[:, :, width:]
        return jnp.where(position < mine, longer, state)

    state = lax.fori_loop(0, count - 1, lap, jnp.zeros_like(offset))
    core = near + batched3(reach, state)
    mean_sq = jnp.mean(core * core, axis=-1, keepdims=True)
    normed = (core * lax.rsqrt(mean_sq + norm_eps) * norm_gain).astype(bf16)
    flat = jnp.transpose(normed, (1, 0, 2)).reshape(length, -1)
    mixed = lax.psum_scatter(
        jnp.dot(flat, w_out, preferred_element_type=f32), "heads", scatter_dimension=0, tiled=True
    )
    return mixed.astype(bf16)


def solution(mesh):
    return jax.shard_map(
        body,
        mesh=mesh,
        in_specs=(
            P("seq", "heads", None),
            P("seq", "heads", None),
            P("seq", "heads", None),
            P("seq", "heads"),
            P("seq", "heads"),
            P(),
            P("heads", None),
        ),
        out_specs=P(("seq", "heads"), None),
        check_vma=False,
    )
```

time: 413 us -> 162 us (0.39)
  other arithmetic: 174 us -> 4.37 us
  matrix products: 81.9 us -> 10.6 us
  waiting for transfers between devices: 119 us -> 98.4 us
  Pallas kernels: 0 us -> 14.3 us
    another operation x26 -> x0, other arithmetic: 164 us -> none  [the longest x16 163 us: block_parts(): jax.scipy.linalg.solve_triangular(system, right_side, lower=True, unit_di...]
    dot_general x48 -> x25, matrix products: 75.5 us -> 10.6 us  [the longest x24 5.82 us: batched3(): jnp.einsum('hik,hkj->hij', x, y, preferred_element_type=f32)]
    all_gather x2 -> x1, waiting for transfers between devices: 74.5 us -> 54.4 us  [body(): maps = lax.all_gather(jnp.concatenate([transit, offset], axis=2), 'seq')]
    pallas_call x0 -> x1, Pallas kernels: none -> 14.3 us  [local_phase(): pl.pallas_call(functools.partial(local_kernel, group_size), grid=(heads_k...]
    dynamic_slice x28 -> x0, local copies, waits for them, and re-layouts: 11 us -> none  [the longest x20 10.7 us: body(): lax.scan(analyse, jnp.zeros((), jnp.float32), blocks)]
    squeeze x0 -> x7, local copies, waits for them, and re-layouts: none -> 9.18 us  [lap(): pair = maps[position]]
    another operation x4 -> x0, matrix products: 6.39 us -> none  [block_parts(): jax.scipy.linalg.solve_triangular(system, right_side, lower=True, unit_di...]
    unnamed x6 -> x9, local copies, waits for them, and re-layouts: 0.89 us -> 5.55 us
  transfers between devices with their start and end apart: 3 -> 2, of which waited for: 3 -> 2; matrix products, arithmetic and copies ran while one was open for 0% -> 0% of each run, Pallas kernels for 0% -> 0%
where the time goes in v1:
time: 162 us; the launch traced here: 159 us
  waiting for transfers between devices  98.4 us (61%)
  local copies, waits for them, and re-layouts  17.1 us (11%)
  Pallas kernels  14.3 us (9%)
  between operations  13.5 us (8%)
  matrix products  10.6 us (7%)
  other arithmetic  4.37 us (3%)
    all_gather x1, waiting for transfers between devices, body(): maps = lax.all_gather(jnp.concatenate([transit, offset], axis=2), 'seq')  54.4 us
    reduce_scatter x1, waiting for transfers between devices, body(): lax.psum_scatter(jnp.dot(flat, w_out, preferred_element_type=f32), 'heads...  43.9 us
    pallas_call x1, Pallas kernels, local_phase(): pl.pallas_call(functools.partial(local_kernel, group_size), grid=(heads_k...  14.3 us
    squeeze x7, local copies, waits for them, and re-layouts, lap(): pair = maps[position]  9.18 us
    dot_general x24, matrix products, batched3(): jnp.einsum('hik,hkj->hij', x, y, preferred_element_type=f32)  5.82 us
    unnamed x9, local copies, waits for them, and re-layouts  5.55 us
    dot_general x1, matrix products, body(): jnp.dot(flat, w_out, preferred_element_type=f32)  4.81 us
  transfers between devices with their start and end apart: 2, of which 2 were waited for; matrix products, arithmetic and copies ran while one was open for 0% of the time, Pallas kernels for 0%

profile of v1, /device:TPU:22, one launch (start us, length us, event | category | flops | bytes accessed | tf_op | source)
XLA Modules:
  0.0 158.6 jit_solution(14412759569752910757)
XLA Ops:
  6.5 1.5 copy.25.strength_ref
  8.0 1.5 copy.26.decay_ref
  9.5 2.0 %copy.46 = bf16[32,8,8,128]{3,1,2,0:T(8,128)(2,1)} copy(bf16[32,8,8,128]{3,2,1,0:T(8,128)(2,1)} %bitcast.22) | data formatting | bytes 1048576
  11.5 1.9 %copy_bitcast_fusion.1 = (bf16[256,512]{1,0:T(8,128)(2,1)}, bf16[256,512]{1,0:T(8,128)(2,1)}) fusion(bf16[32,8,4,128]{3,2,1,0:T(4,128)(2,1)} %bitcast.24, bf16[32,8,4,128]{3,2,1,0:T(4,128)(2,1)} %bitcast.25), kind=kLoop, calls=%fused_computation.31 | loop fusion | bytes 1048576 | tf_op jit(solution)/shard_map/reshape | solution.py:191
  13.3 14.3 %local_phase.1 = (f32[8,128,128]{2,1,0:T(8,128)}, f32[8,128,128]{2,1,0:T(8,128)}, f32[8,256,128]{2,1,0:T(8,128)}, f32[8,256,128]{2,1,0:T(8,128)}) custom-call(bf16[256,512]{1,0:T(8,128)(2,1)} %get-tuple-element.119.q_ref, bf16[256,512]{1,0:T(8,128)(2,1)} %get-tuple-element.118.k_ref, bf16[256,1024]{1,0:T(8,128)(2,1)} %bitcast.21, ...), custom_call_target="tpu_custom_call" | custom-call | tf_op jit(solution)/shard_map/local_phase/pallas_call | solution.py:176
  27.6 2.3 %pad_maximum_fusion = f32[8,128,256]{2,1,0:T(8,128)} fusion(f32[8,128,128]{2,1,0:T(8,128)} %get-tuple-element.91, f32[8,128,128]{2,1,0:T(8,128)} %get-tuple-element.90), kind=kLoop, calls=%fused_computation.23 | loop fusion | flops 262144 | bytes 2097152 | tf_op jit(solution)/shard_map/concatenate | solution.py:208
  29.8 0.0 all-gather.3.cloned.1.call-update
  29.9 0.0 reduce-scatter.2.cloned.1.call-start
  29.9 54.4 %all-gather.3.cloned.1.call-done = f32[64,128,256]{2,1,0:T(8,128)} async-done(((f32[8,128,256]{2,1,0:T(8,128)}), f32[64,128,256]{2,1,0:T(8,128)}) %all-gather.3.cloned.1.call-update) | async-done | bytes 8388624 | tf_op jit(solution)/shard_map/all_gather | solution.py:208
  84.4 14.5 %while.14 = (s32[]{:T(128)}, f32[8,128,128]{2,1,0:T(8,128)S(1)}, s32[]{:T(128)}, f32[8,8,128,256]{3,2,1,0:T(8,128)}, s32[]{:T(128)}, /*index=5*/s32[]{:T(128)}) while((s32[]{:T(128)}, f32[8,128,128]{2,1,0:T(8,128)S(1)}, s32[]{:T(128)}, f32[8,8,128,256]{3,2,1,0:T(8,128)}, s32[]{:T(128)}, /*index=5*/s32[]{:T(128)}) %tuple.41), condition=%wide.region_1.2_spmd.clone, body=%wide.region_0.1_spmd.clone.sunk | while | flops 102891520 | bytes 9438821 | solution.py:216
  84.4 1.4 dynamic-slice_bitcast_fusion.2
  85.8 0.2 fusion.32
  86.0 0.2 fusion.31
  86.2 0.2 fusion.33
  86.5 1.3 dynamic-slice_bitcast_fusion.2
  87.9 0.2 fusion.32
  88.1 0.2 fusion.31
  88.3 0.2 fusion.33
  88.6 1.3 dynamic-slice_bitcast_fusion.2
  89.9 0.2 fusion.32
  90.1 0.2 fusion.31
  90.4 0.2 fusion.33
  90.7 1.3 dynamic-slice_bitcast_fusion.2
  92.0 0.2 fusion.32
  92.2 0.2 fusion.31
  92.4 0.2 fusion.33
  92.7 1.3 dynamic-slice_bitcast_fusion.2
  94.1 0.2 fusion.32
  94.3 0.2 fusion.31
  94.5 0.2 fusion.33
  94.8 1.3 dynamic-slice_bitcast_fusion.2
  96.1 0.2 fusion.32
  96.3 0.2 fusion.31
  96.6 0.2 fusion.33
  96.9 1.3 dynamic-slice_bitcast_fusion.2
  98.2 0.2 fusion.32
  98.4 0.2 fusion.31
  98.6 0.2 fusion.33
  98.9 0.3 fusion.17
  99.2 0.3 fusion.20
  99.5 0.6 copy-done.1
  100.1 0.5 multiply_reduce_fusion
  100.7 0.3 fusion.16
  101.0 0.2 copy.33
  101.2 4.8 %fusion.25 = f32[256,2048]{1,0:T(8,128)} fusion(bf16[256,1024]{0,1:T(8,128)(2,1)S(1)} %bitcast.23, bf16[1024,2048]{1,0:T(8,128)(2,1)} %param.15), kind=kOutput, calls=%fused_computation.41 | convolution fusion | flops 1073741824 | bytes 6815744 | tf_op jit(solution)/shard_map/dot_general | solution.py:222
  106.0 0.0 reduce-scatter.2.cloned.1.call-update
  106.1 43.9 %reduce-scatter.2.cloned.1.call-done = f32[64,2048]{1,0:T(8,128)} async-done(((f32[256,2048]{1,0:T(8,128)}), f32[64,2048]{1,0:T(8,128)}) %reduce-scatter.2.cloned.1.call-update) | async-done | bytes 524304 | tf_op jit(solution)/shard_map/reduce_scatter | solution.py:221
  150.0 1.8 %convert_element_type.73 = bf16[64,2048]{1,0:T(8,128)(2,1)} convert(f32[64,2048]{1,0:T(8,128)} %reduce-scatter.2.cloned.1.call-done) | non-fusion elementwise | flops 131072 | bytes 786432 | tf_op jit(solution)/shard_map/convert_element_type | solution.py:224
  (15 shorter events, 0.3 us)
Async XLA Ops:
  6.5 77.8 %all-gather.3.cloned.1.call-start = ((), (), s32[]{:S(2)}) async-start(), calls=%async_computation.2 | async-start | bytes 9437184 | tf_op jit(solution)/shard_map/all_gather | solution.py:208
  29.9 120.1 %reduce-scatter.2.cloned.1.call-start = ((), (), s32[]{:S(2)}) async-start(), calls=%async_computation.1 | async-start | bytes 2621440 | tf_op jit(solution)/shard_map/reduce_scatter | solution.py:221
  84.4 14.5 %copy-start = (f32[8,256,128]{2,1,0:T(8,128)S(1)}, f32[8,256,128]{2,1,0:T(8,128)}, u32[]{:S(2)}) copy-start(f32[8,256,128]{2,1,0:T(8,128)} %get-tuple-element.89) | copy-start | bytes 3145732
  98.9 1.2 copy-start.1
  99.2 1.5 copy-start.2
Sparse Core Ops, SparseCore 0:
  30.0 54.3 all-gather.2
  106.2 43.7 reduce-scatter.1

commit v2 on v1

--- a/solution.py
+++ b/solution.py
@@ -195,38 +195,208 @@
     )
 
 
-def batched3(a, b):
-    one = lambda x, y: jnp.einsum("hik,hkj->hij", x, y, preferred_element_type=f32)
-    a, b = split(a), split(b)
-    return one(a[0], b[0]) + (one(a[0], b[1]) + one(a[1], b[0]))
-
-
-def body(queries, key_vecs, values, strength, decay_rate, norm_gain, w_out):
-    length = queries.shape[0]
-    transit, offset, reach, near = local_phase(queries, key_vecs, values, strength, decay_rate)
-    count, mine = lax.axis_size("seq"), lax.axis_index("seq")
-    maps = lax.all_gather(jnp.concatenate([transit, offset], axis=2), "seq")
-    width = transit.shape[1]
-
-    def lap(position, state):
-        pair = maps[position]
-        longer = batched3(pair[:, :, :width], state) + pair[:, :, width:]
-        return jnp.where(position < mine, longer, state)
-
-    state = lax.fori_loop(0, count - 1, lap, jnp.zeros_like(offset))
-    core = near + batched3(reach, state)
-    mean_sq = jnp.mean(core * core, axis=-1, keepdims=True)
-    normed = (core * lax.rsqrt(mean_sq + norm_eps) * norm_gain).astype(bf16)
-    flat = jnp.transpose(normed, (1, 0, 2)).reshape(length, -1)
-    mixed = lax.psum_scatter(
-        jnp.dot(flat, w_out, preferred_element_type=f32), "heads", scatter_dimension=0, tiled=True
+MESH = pl.DeviceIdType.MESH
+PIECES = 4
+
+
+def finish_kernel(
+    np_seq,
+    np_heads,
+    transit_ref,
+    offset_ref,
+    reach_ref,
+    near_ref,
+    gain_ref,
+    w_hbm,
+    out_ref,
+    w_ref,
+    state_ref,
+    next_ref,
+    normed_ref,
+    part_ref,
+    right_ref,
+    left_ref,
+    w_sem,
+    state_send,
+    state_recv,
+    right_send,
+    right_recv,
+    left_send,
+    left_recv,
+):
+    p, m = lax.axis_index("seq"), lax.axis_index("heads")
+    heads, length, width = near_ref.shape
+    rows = length // np_heads
+    columns = out_ref.shape[1]
+    piece = columns // PIECES
+
+    load = pltpu.make_async_copy(w_hbm, w_ref, w_sem)
+    load.start()
+
+    barrier = pltpu.get_barrier_semaphore()
+    neighbours = (
+        {"seq": lax.rem(p + 1, np_seq)},
+        {"seq": lax.rem(p + np_seq - 1, np_seq)},
+        {"heads": lax.rem(m + 1, np_heads)},
+        {"heads": lax.rem(m + np_heads - 1, np_heads)},
     )
-    return mixed.astype(bf16)
+    for where in neighbours:
+        pl.semaphore_signal(barrier, inc=1, device_id=where, device_id_type=MESH)
+    pl.semaphore_wait(barrier, len(neighbours))
+
+    def hop(h):
+        return pltpu.make_async_remote_copy(
+            src_ref=next_ref.at[h],
+            dst_ref=state_ref.at[h],
+            send_sem=state_send.at[h],
+            recv_sem=state_recv.at[h],
+            device_id={"seq": p + 1},
+            device_id_type=MESH,
+        )
+
+    @pl.when(p == 0)
+    def _():
+        state_ref[...] = jnp.zeros_like(state_ref)
+
+    @pl.loop(0, heads)
+    def _(h):
+        transit = split(transit_ref[h])
+
+        @pl.when(p > 0)
+        def _():
+            hop(h).wait_recv()
+
+        @pl.when(p < np_seq - 1)
+        def _():
+            next_ref[h] = mm3(transit, split(state_ref[h])) + offset_ref[h]
+            hop(h).start()
+
+    for h in range(heads):
+        core = near_ref[h] + mm3(split(reach_ref[h]), split(state_ref[h]))
+        mean_sq = jnp.mean(core * core, axis=1, keepdims=True)
+        normed = core * lax.rsqrt(mean_sq + norm_eps) * gain_ref[...]
+        normed_ref[:, h * width : (h + 1) * width] = normed.astype(bf16)
+    load.wait()
+
+    def flow(buffer, send, recv, d, c, target):
+        return pltpu.make_async_remote_copy(
+            src_ref=part_ref.at[d, c],
+            dst_ref=buffer.at[d, c],
+            send_sem=send.at[d, c],
+            recv_sem=recv.at[d, c],
+            device_id={"heads": target},
+            device_id_type=MESH,
+        )
+
+    right = lambda d, c: flow(right_ref, right_send, right_recv, d, c, m + 1)
+    left = lambda d, c: flow(left_ref, left_send, left_recv, d, c, m - 1)
+
+    def pass_on(d, c):
+        if d > 0:
+
+            @pl.when(m < d)
+            def _():
+                @pl.when(m > 0)
+                def _():
+                    right(d, c).wait_recv()
+                    part_ref[d, c] += right_ref[d, c]
+
+                right(d, c).start()
+
+        if d < np_heads - 1:
+
+            @pl.when(m > d)
+            def _():
+                @pl.when(m < np_heads - 1)
+                def _():
+                    left(d, c).wait_recv()
+                    part_ref[d, c] += left_ref[d, c]
+
+                left(d, c).start()
+
+    order = []
+    for i in range(np_heads):
+        group = [d for d in dict.fromkeys((np_heads - 1 - i, i)) if d not in sum(order, [])]
+        if group:
+            order.append(group)
+    for group in order:
+        for c in range(PIECES):
+            for d in group:
+                part_ref[d, c] = mm(
+                    normed_ref[d * rows : (d + 1) * rows, :],
+                    w_ref[:, c * piece : (c + 1) * piece],
+                )
+        for c in range(PIECES):
+            for d in group:
+                pass_on(d, c)
+
+    for c in range(PIECES):
+
+        @pl.when(m > 0)
+        def _():
+            right(m, c).wait_recv()
+            part_ref[m, c] += right_ref[m, c]
+
+        @pl.when(m < np_heads - 1)
+        def _():
+            left(m, c).wait_recv()
+            part_ref[m, c] += left_ref[m, c]
+
+        out_ref[:, c * piece : (c + 1) * piece] = part_ref[m, c].astype(bf16)
+
+    @pl.when(p < np_seq - 1)
+    def _():
+        for h in range(heads):
+            hop(h).wait_send()
+
+    for d in range(np_heads):
+        for c in range(PIECES):
+            if d > 0:
+
+                @pl.when(m < d)
+                def _():
+                    right(d, c).wait_send()
+
+            if d < np_heads - 1:
+
+                @pl.when(m > d)
+                def _():
+                    left(d, c).wait_send()
+
+
+def finish(np_seq, np_heads, transit, offset, reach, near, norm_gain, w_out):
+    heads, length, width = near.shape
+    columns = w_out.shape[1]
+    rows = length // np_heads
+    vmem = pl.BlockSpec(memory_space=pltpu.VMEM)
+    slots = (np_heads, PIECES)
+    dma = pltpu.SemaphoreType.DMA
+    return pl.pallas_call(
+        functools.partial(finish_kernel, np_seq, np_heads),
+        out_shape=jax.ShapeDtypeStruct((rows, columns), bf16),
+        in_specs=[vmem] * 5 + [pl.BlockSpec(memory_space=pl.ANY)],
+        out_specs=vmem,
+        scratch_shapes=[
+            pltpu.VMEM(w_out.shape, bf16),
+            pltpu.VMEM((heads, width, width), f32),
+            pltpu.VMEM((heads, width, width), f32),
+            pltpu.VMEM((length, heads * width), bf16),
+        ]
+        + [pltpu.VMEM(slots + (rows, columns // PIECES), f32)] * 3
+        + [dma, dma((heads,)), dma((heads,)), dma(slots), dma(slots), dma(slots), dma(slots)],
+        compiler_params=pltpu.CompilerParams(collective_id=0, has_side_effects=True),
+        name="finish",
+    )(transit, offset, reach, near, norm_gain.reshape(1, width), w_out)
+
+
+def body(np_seq, np_heads, queries, key_vecs, values, strength, decay_rate, norm_gain, w_out):
+    maps = local_phase(queries, key_vecs, values, strength, decay_rate)
+    return finish(np_seq, np_heads, *maps, norm_gain, w_out)
 
 
 def solution(mesh):
     return jax.shard_map(
-        body,
+        functools.partial(body, mesh.shape["seq"], mesh.shape["heads"]),
         mesh=mesh,
         in_specs=(
             P("seq", "heads", None),

time: 162 us -> 99.4 us (0.61); the launches traced: 159 us -> 99 us
  waiting for transfers between devices: 98.4 us -> 0 us
  Pallas kernels: 14.3 us -> 90.6 us
  between operations: 13.5 us -> 0.01 us
  matrix products: 10.6 us -> 0 us
  local copies, waits for them, and re-layouts: 17.1 us -> 8.41 us
  other arithmetic: 4.37 us -> 0 us
    pallas_call x0 -> x1, Pallas kernels: none -> 76.4 us  [finish(): pl.pallas_call(functools.partial(finish_kernel, np_seq, np_heads), out_sh...]
    all_gather x1 -> x0, waiting for transfers between devices: 54.4 us -> none  [body(): maps = lax.all_gather(jnp.concatenate([transit, offset], axis=2), 'seq')]
    reduce_scatter x1 -> x0, waiting for transfers between devices: 43.9 us -> none  [body(): lax.psum_scatter(jnp.dot(flat, w_out, preferred_element_type=f32), 'heads...]
    dot_general x25 -> x0, matrix products: 10.6 us -> none  [the longest x24 5.82 us: batched3(): jnp.einsum('hik,hkj->hij', x, y, preferred_element_type=f32)]
    squeeze x7 -> x0, local copies, waits for them, and re-layouts: 9.18 us -> none  [lap(): pair = maps[position]]
    concatenate x1 -> x0, other arithmetic: 2.26 us -> none  [body(): maps = lax.all_gather(jnp.concatenate([transit, offset], axis=2), 'seq')]
    convert_element_type x1 -> x0, other arithmetic: 1.77 us -> none  [body(): return mixed.astype(bf16)]
    unnamed x9 -> x4, local copies, waits for them, and re-layouts: 5.55 us -> 6.54 us
  transfers between devices with their start and end apart: 2 -> 0, of which waited for: 2 -> 0; matrix products, arithmetic and copies ran while one was open for 0% -> 0% of each run, Pallas kernels for 0% -> 0%
where the time goes in v2:
time: 99.4 us; the launch traced here: 99 us
  Pallas kernels  90.6 us (91%)
  local copies, waits for them, and re-layouts  8.41 us (8%)
    pallas_call x1, Pallas kernels, finish(): pl.pallas_call(functools.partial(finish_kernel, np_seq, np_heads), out_sh...  76.4 us
    pallas_call x1, Pallas kernels, local_phase(): pl.pallas_call(functools.partial(local_kernel, group_size), grid=(heads_k...  14.2 us
    unnamed x4, local copies, waits for them, and re-layouts  6.54 us

profile of v2, /device:TPU:22, one launch (start us, length us, event | category | flops | bytes accessed | tf_op | source)
XLA Modules:
  0.0 99.0 jit_solution(5633019116967463690)
XLA Ops:
  0.0 1.5 %copy.8.strength_ref = f32[256,8]{1,0:T(8,128)} copy(f32[256,8]{0,1:T(8,128)} %param.10) | data formatting | bytes 16384 | tf_op args[3]
  1.5 1.5 %copy.9.decay_ref = f32[256,8]{1,0:T(8,128)} copy(f32[256,8]{0,1:T(8,128)} %param.11) | data formatting | bytes 16384 | tf_op args[4]
  2.9 1.9 %copy.16 = bf16[32,8,8,128]{3,1,2,0:T(8,128)(2,1)} copy(bf16[32,8,8,128]{3,2,1,0:T(8,128)(2,1)} %bitcast.12) | data formatting | bytes 1048576
  4.9 1.9 %copy_bitcast_fusion.1 = (bf16[256,512]{1,0:T(8,128)(2,1)}, bf16[256,512]{1,0:T(8,128)(2,1)}) fusion(bf16[32,8,4,128]{3,2,1,0:T(4,128)(2,1)} %bitcast.13, bf16[32,8,4,128]{3,2,1,0:T(4,128)(2,1)} %bitcast.14), kind=kLoop, calls=%fused_computation.1 | loop fusion | bytes 1048576 | tf_op jit(solution)/shard_map/reshape | solution.py:191
  6.7 14.2 %local_phase.1 = (f32[8,128,128]{2,1,0:T(8,128)}, f32[8,128,128]{2,1,0:T(8,128)}, f32[8,256,128]{2,1,0:T(8,128)}, f32[8,256,128]{2,1,0:T(8,128)}) custom-call(bf16[256,512]{1,0:T(8,128)(2,1)} %get-tuple-element.14.q_ref, bf16[256,512]{1,0:T(8,128)(2,1)} %get-tuple-element.13.k_ref, bf16[256,1024]{1,0:T(8,128)(2,1)} %bitcast.11, f32[256,8]{1,0:T(8,128)} %copy.8.strength_ref, ...), custom_call_target="tpu_custom_call" | custom-call | tf_op jit(solution)/shard_map/local_phase/pallas_call | solution.py:176
  21.0 76.4 %finish.1 = bf16[64,2048]{1,0:T(8,128)(2,1)} custom-call(f32[8,128,128]{2,1,0:T(8,128)} %get-tuple-element.9.transit_ref, f32[8,128,128]{2,1,0:T(8,128)} %get-tuple-element.10.offset_ref, f32[8,256,128]{2,1,0:T(8,128)} %get-tuple-element.11.reach_ref, f32[8,256,128]{2,1,0:T(8,128)} %get-tuple-element.12.near_ref, f32[1,128]{1,0:T(1,128)} %bitcast.15, ...), custom_call_target="tpu_custom_call" | custom-call | tf_op jit(solution)/shard_map/finish/pallas_call | solution.py:374
  97.4 1.7 %copy.18 = bf16[64,2048]{1,0:T(8,128)(2,1)} copy(bf16[64,2048]{1,0:T(8,128)(2,1)} %finish.1) | data formatting | bytes 524288

commit v3 on v2

--- a/solution.py
+++ b/solution.py
@@ -86,7 +86,7 @@
 ):
     step = pl.program_id(0)
     length = q_ref.shape[0]
-    heads = decay_ref.shape[1]
+    heads = decay_ref.shape[0]
     width = k_ref.shape[1]
     query, key = q_ref[...], k_ref[...]
     query_f, key_f = query.astype(f32), key.astype(f32)
@@ -101,8 +101,11 @@
     lower = jnp.where(row >= col, 1.0, 0.0).astype(bf16)
     upper = jnp.where(row <= col, 1.0, 0.0).astype(bf16)
     pieces = split3(-decay_ref[...])
-    logs = mm(lower, pieces[0]) + (mm(lower, pieces[1]) + mm(lower, pieces[2]))
-    logs_row = mm(pieces[0], upper, TN) + (mm(pieces[1], upper, TN) + mm(pieces[2], upper, TN))
+    logs = mm(lower, pieces[0], NT) + (mm(lower, pieces[1], NT) + mm(lower, pieces[2], NT))
+    logs_row = mm(pieces[0], upper) + (mm(pieces[1], upper) + mm(pieces[2], upper))
+    same = jnp.where(row == col, 1.0, 0.0).astype(bf16)
+    strong = split3(strength_ref[...])
+    strengths = mm(same, strong[0], NT) + (mm(same, strong[1], NT) + mm(same, strong[2], NT))
 
     key_dots = mm(key, key, NT) * key_scale * key_scale_row
     query_dots = mm(query, key, NT) * query_scale * key_scale_row
@@ -113,7 +116,7 @@
         head = step * group_size + n
         lane = iota((length, heads), 1)
         log_col = jnp.sum(jnp.where(lane == head, logs, 0.0), axis=1, keepdims=True)
-        write = jnp.sum(jnp.where(lane == head, strength_ref[...], 0.0), axis=1, keepdims=True)
+        write = jnp.sum(jnp.where(lane == head, strengths, 0.0), axis=1, keepdims=True)
         log_row = jnp.sum(
             jnp.where(iota((heads, length), 0) == head, logs_row, 0.0), axis=0, keepdims=True
         )
@@ -172,7 +175,7 @@
     group_size = heads_v // heads_k
     per_head = lambda rows: pl.BlockSpec((group_size, rows, width), lambda i: (i, 0, 0))
     lanes = lambda n: pl.BlockSpec((length, n * width), lambda i: (0, i))
-    whole = pl.BlockSpec((length, heads_v), lambda i: (0, 0))
+    whole = pl.BlockSpec((heads_v, length), lambda i: (0, 0))
     return pl.pallas_call(
         functools.partial(local_kernel, group_size),
         grid=(heads_k,),
@@ -190,13 +193,13 @@
         queries.reshape(length, heads_k * width),
         key_vecs.reshape(length, heads_k * width),
         values.reshape(length, heads_v * width),
-        strength,
-        decay_rate,
+        jnp.transpose(strength),
+        jnp.transpose(decay_rate),
     )
 
 
 MESH = pl.DeviceIdType.MESH
-PIECES = 4
+PIECES = 8
 
 
 def finish_kernel(
@@ -291,44 +294,41 @@
     right = lambda d, c: flow(right_ref, right_send, right_recv, d, c, m + 1)
     left = lambda d, c: flow(left_ref, left_send, left_recv, d, c, m - 1)
 
-    def pass_on(d, c):
-        if d > 0:
-
-            @pl.when(m < d)
+    def pass_right(d, c):
+        @pl.when(m < d)
+        def _():
+            @pl.when(m > 0)
             def _():
-                @pl.when(m > 0)
-                def _():
-                    right(d, c).wait_recv()
-                    part_ref[d, c] += right_ref[d, c]
-
-                right(d, c).start()
-
-        if d < np_heads - 1:
-
-            @pl.when(m > d)
+                right(d, c).wait_recv()
+                part_ref[d, c] += right_ref[d, c]
+
+            right(d, c).start()
+
+    def pass_left(d, c):
+        @pl.when(m > d)
+        def _():
+            @pl.when(m < np_heads - 1)
             def _():
-                @pl.when(m < np_heads - 1)
-                def _():
-                    left(d, c).wait_recv()
-                    part_ref[d, c] += left_ref[d, c]
-
-                left(d, c).start()
-
-    order = []
+                left(d, c).wait_recv()
+                part_ref[d, c] += left_ref[d, c]
+
+            left(d, c).start()
+
+    ready = []
     for i in range(np_heads):
-        group = [d for d in dict.fromkeys((np_heads - 1 - i, i)) if d not in sum(order, [])]
-        if group:
-            order.append(group)
-    for group in order:
-        for c in range(PIECES):
-            for d in group:
-                part_ref[d, c] = mm(
-                    normed_ref[d * rows : (d + 1) * rows, :],
-                    w_ref[:, c * piece : (c + 1) * piece],
-                )
-        for c in range(PIECES):
-            for d in group:
-                pass_on(d, c)
+        far = np_heads - 1 - i
+        for d in (far, i):
+            if d not in ready:
+                ready.append(d)
+                for c in range(PIECES):
+                    part_ref[d, c] = mm(
+                        normed_ref[d * rows : (d + 1) * rows, :],
+                        w_ref[:, c * piece : (c + 1) * piece],
+                    )
+        if far:
+            for c in range(PIECES):
+                pass_right(far, c)
+                pass_left(i, c)
 
     for c in range(PIECES):
 

time: 99.4 us -> 114 us (1.15)
  Pallas kernels: 90.6 us -> 108 us
  local copies, waits for them, and re-layouts: 8.41 us -> 5.47 us
    pallas_call x1, Pallas kernels: 76.4 us -> 94.3 us  [finish(): pl.pallas_call(functools.partial(finish_kernel, np_seq, np_heads), out_sh...]
    unnamed x4 -> x2, local copies, waits for them, and re-layouts: 6.54 us -> 3.6 us
where the time goes in v3:
time: 114 us
  Pallas kernels  108 us (95%)
  local copies, waits for them, and re-layouts  5.47 us (5%)
    pallas_call x1, Pallas kernels, finish(): pl.pallas_call(functools.partial(finish_kernel, np_seq, np_heads), out_sh...  94.3 us
    pallas_call x1, Pallas kernels, local_phase(): pl.pallas_call(functools.partial(local_kernel, group_size), grid=(heads_k...  14.2 us
    unnamed x2, local copies, waits for them, and re-layouts  3.6 us

profile of v3, /device:TPU:22, one launch (start us, length us, event | category | flops | bytes accessed | tf_op | source)
XLA Modules:
  0.0 113.9 jit_solution(2427862633251533968)
XLA Ops:
  0.0 1.9 %copy.14 = bf16[32,8,8,128]{3,1,2,0:T(8,128)(2,1)} copy(bf16[32,8,8,128]{3,2,1,0:T(8,128)(2,1)} %bitcast.14) | data formatting | bytes 1048576
  1.9 1.9 %copy_bitcast_fusion.1 = (bf16[256,512]{1,0:T(8,128)(2,1)}, bf16[256,512]{1,0:T(8,128)(2,1)}) fusion(bf16[32,8,4,128]{3,2,1,0:T(4,128)(2,1)} %bitcast.15, bf16[32,8,4,128]{3,2,1,0:T(4,128)(2,1)} %bitcast.16), kind=kLoop, calls=%fused_computation.1 | loop fusion | bytes 1048576 | tf_op jit(solution)/shard_map/reshape | solution.py:194
  3.8 14.2 %local_phase.1 = (f32[8,128,128]{2,1,0:T(8,128)}, f32[8,128,128]{2,1,0:T(8,128)}, f32[8,256,128]{2,1,0:T(8,128)}, f32[8,256,128]{2,1,0:T(8,128)}) custom-call(bf16[256,512]{1,0:T(8,128)(2,1)} %get-tuple-element.14.q_ref, bf16[256,512]{1,0:T(8,128)(2,1)} %get-tuple-element.13.k_ref, bf16[256,1024]{1,0:T(8,128)(2,1)} %bitcast.13, f32[8,256]{1,0:T(8,128)} %bitcast.17, ...), custom_call_target="tpu_custom_call" | custom-call | tf_op jit(solution)/shard_map/local_phase/pallas_call | solution.py:179
  18.0 94.3 %finish.1 = bf16[64,2048]{1,0:T(8,128)(2,1)} custom-call(f32[8,128,128]{2,1,0:T(8,128)} %get-tuple-element.9.transit_ref, f32[8,128,128]{2,1,0:T(8,128)} %get-tuple-element.10.offset_ref, f32[8,256,128]{2,1,0:T(8,128)} %get-tuple-element.11.reach_ref, f32[8,256,128]{2,1,0:T(8,128)} %get-tuple-element.12.near_ref, f32[1,128]{1,0:T(1,128)} %bitcast.19, ...), custom_call_target="tpu_custom_call" | custom-call | tf_op jit(solution)/shard_map/finish/pallas_call | solution.py:374
  112.3 1.7 %copy.16 = bf16[64,2048]{1,0:T(8,128)(2,1)} copy(bf16[64,2048]{1,0:T(8,128)(2,1)} %finish.1) | data formatting | bytes 524288

commit v4 on v3

--- a/solution.py
+++ b/solution.py
@@ -199,7 +199,7 @@
 
 
 MESH = pl.DeviceIdType.MESH
-PIECES = 8
+PIECES = 2
 
 
 def finish_kernel(

time: 114 us -> 96.7 us (0.85)
  Pallas kernels: 108 us -> 91 us
    pallas_call x1, Pallas kernels: 94.3 us -> 76.8 us  [finish(): pl.pallas_call(functools.partial(finish_kernel, np_seq, np_heads), out_sh...]
where the time goes in v4:
time: 96.7 us; the launch traced here: 96.4 us
  Pallas kernels  91 us (94%)
  local copies, waits for them, and re-layouts  5.47 us (6%)
    pallas_call x1, Pallas kernels, finish(): pl.pallas_call(functools.partial(finish_kernel, np_seq, np_heads), out_sh...  76.8 us
    pallas_call x1, Pallas kernels, local_phase(): pl.pallas_call(functools.partial(local_kernel, group_size), grid=(heads_k...  14.2 us
    unnamed x2, local copies, waits for them, and re-layouts  3.6 us

profile of v4, /device:TPU:22, one launch (start us, length us, event | category | flops | bytes accessed | tf_op | source)
XLA Modules:
  0.0 96.4 jit_solution(4116075952690041786)
XLA Ops:
  0.0 1.9 %copy.14 = bf16[32,8,8,128]{3,1,2,0:T(8,128)(2,1)} copy(bf16[32,8,8,128]{3,2,1,0:T(8,128)(2,1)} %bitcast.14) | data formatting | bytes 1048576
  1.9 1.9 %copy_bitcast_fusion.1 = (bf16[256,512]{1,0:T(8,128)(2,1)}, bf16[256,512]{1,0:T(8,128)(2,1)}) fusion(bf16[32,8,4,128]{3,2,1,0:T(4,128)(2,1)} %bitcast.15, bf16[32,8,4,128]{3,2,1,0:T(4,128)(2,1)} %bitcast.16), kind=kLoop, calls=%fused_computation.1 | loop fusion | bytes 1048576 | tf_op jit(solution)/shard_map/reshape | solution.py:194
  3.8 14.2 %local_phase.1 = (f32[8,128,128]{2,1,0:T(8,128)}, f32[8,128,128]{2,1,0:T(8,128)}, f32[8,256,128]{2,1,0:T(8,128)}, f32[8,256,128]{2,1,0:T(8,128)}) custom-call(bf16[256,512]{1,0:T(8,128)(2,1)} %get-tuple-element.14.q_ref, bf16[256,512]{1,0:T(8,128)(2,1)} %get-tuple-element.13.k_ref, bf16[256,1024]{1,0:T(8,128)(2,1)} %bitcast.13, f32[8,256]{1,0:T(8,128)} %bitcast.17, ...), custom_call_target="tpu_custom_call" | custom-call | tf_op jit(solution)/shard_map/local_phase/pallas_call | solution.py:179
  18.0 76.8 %finish.1 = bf16[64,2048]{1,0:T(8,128)(2,1)} custom-call(f32[8,128,128]{2,1,0:T(8,128)} %get-tuple-element.9.transit_ref, f32[8,128,128]{2,1,0:T(8,128)} %get-tuple-element.10.offset_ref, f32[8,256,128]{2,1,0:T(8,128)} %get-tuple-element.11.reach_ref, f32[8,256,128]{2,1,0:T(8,128)} %get-tuple-element.12.near_ref, f32[1,128]{1,0:T(1,128)} %bitcast.19, ...), custom_call_target="tpu_custom_call" | custom-call | tf_op jit(solution)/shard_map/finish/pallas_call | solution.py:374
  94.8 1.7 %copy.16 = bf16[64,2048]{1,0:T(8,128)(2,1)} copy(bf16[64,2048]{1,0:T(8,128)(2,1)} %finish.1) | data formatting | bytes 524288
